TPU v7x, 256 devices: a whole 4x4x8 slice. The times are simulated.
256 devices in a mesh: dp: 8 (over x, core), tensor: 32 (over z, y).
Axes of the slice: x: 4, y: 4, z: 8, core: 2. Of those that a mesh axis runs over, the one named last changes fastest.
Arguments:
- hidden: bfloat16 [6144, 4096], P('dp', 'tensor'), may hold values from -2000 to 2000
- out_embed: bfloat16 [65536, 4096], P('tensor', 'dp'), may hold values from -0.3 to 0.3
- labels: int32 [6144], P('dp'), may hold values from 0 to 65535
Outputs:
- token_loss: float32 [6144], P(('dp', 'tensor'))
- mean_loss: float32 [], replicated
All inputs are finite; a program needn't handle non-finite values.
Results may differ from a plain program's by a relative error of at most 0.0003.
Values may be sent and summed in bfloat16 or wider, within the bound.
A program may use at most 128 MiB of HBM per device.

v0:
```python
import jax
import jax.numpy as jnp
from jax import lax
from jax.sharding import Mesh
from jax.sharding import PartitionSpec as P

BLOCK = 512
TENSOR = ("tensor_0", "tensor_1")
DP = ("dp_0", "dp_1")
DP_TENSOR = ("dp_0", "dp_1", "tensor_0", "tensor_1")


def whole_of(shard, axes, dim):
    for axis in reversed(axes):
        shard = lax.all_gather(shard, axis, axis=dim, tiled=True)
    return shard


def side_by_side(arrays, axis, split_dim, concat_dim, along):
    both = jnp.concatenate(arrays, axis=along)
    filled, at, done = (
        lax.all_to_all(both, axis, split_axis=split_dim, concat_axis=concat_dim, tiled=True),
        0,
        [],
    )
    for a in arrays:
        done.append(lax.slice_in_dim(filled, at, at + a.shape[along], axis=along))
        at += a.shape[along]
    return tuple(done)


def one_axis_at_a_time(shard, axes):
    for axis in axes:
        shard = lax.psum(shard, axis)
    return shard


def combine_stats(first, second):
    peak_first, mass_first, label_first = first
    peak_second, mass_second, label_second = second
    peak_value = jnp.maximum(peak_first, peak_second)
    exp_total = mass_first * jnp.exp(peak_first - peak_value) + mass_second * jnp.exp(
        peak_second - peak_value
    )
    return (peak_value, exp_total, label_first + label_second)


def block_stats(logits, first_row, labels):
    peak_value = jnp.max(logits, axis=0)
    exp_total = jnp.sum(jnp.exp(logits - peak_value[None, :]), axis=0)
    row_ids = first_row + lax.broadcasted_iota(jnp.int32, logits.shape, 0)
    label_logit = jnp.sum(
        jnp.where(row_ids == labels[None, :], logits, jnp.zeros_like(logits)), axis=0
    )
    return (peak_value, exp_total, label_logit)


def body(hidden, out_embed, labels):
    full_hidden = whole_of(hidden, TENSOR, 1)
    token_count = full_hidden.shape[0]
    vocab_rows = out_embed.shape[0]
    vocab_offset = lax.axis_index(TENSOR) * vocab_rows
    block_count = vocab_rows // BLOCK
    all_logits = lax.dot_general(
        lax.all_gather(out_embed, DP, axis=1, tiled=True),
        full_hidden,
        (((1,), (1,)), ((), ())),
        preferred_element_type=jnp.float32,
    )
    running_stats = None
    for block_index in range(block_count):
        stats = block_stats(
            all_logits[block_index * BLOCK : (block_index + 1) * BLOCK],
            vocab_offset + block_index * BLOCK,
            labels,
        )
        running_stats = stats if running_stats is None else combine_stats(running_stats, stats)
    groups = lax.axis_size(TENSOR)
    share = token_count // groups
    peak_all, mass_all, label_all = running_stats
    peaks, masses, picked = side_by_side(
        (
            peak_all.reshape(groups, share),
            mass_all.reshape(groups, share),
            label_all.reshape(groups, share),
        ),
        TENSOR,
        0,
        0,
        1,
    )
    peak_value = jnp.max(peaks, axis=0)
    exp_total = jnp.sum(masses * jnp.exp(peaks - peak_value[None, :]), axis=0)
    label_logit = jnp.sum(picked, axis=0)
    token_loss = jnp.log(exp_total) + peak_value - label_logit
    loss_sum = one_axis_at_a_time(jnp.sum(token_loss), DP_TENSOR)
    mean_loss = loss_sum / (share * lax.axis_size(DP) * groups)
    return (token_loss, mean_loss)


def solution(mesh):
    finer = Mesh(mesh.devices.reshape(4, 2, 8, 4), ("dp_0", "dp_1", "tensor_0", "tensor_1"))
    return jax.shard_map(
        body,
        mesh=finer,
        in_specs=(P(DP, TENSOR), P(TENSOR, DP), P(DP)),
        out_specs=(P(DP_TENSOR), P()),
        check_vma=False,
    )
```

profile of v0, /device:TPU:32, one launch (start us, length us, event | category | flops | bytes accessed | tf_op | source)
XLA Modules:
  0.0 282.1 jit_solution(3417769360817746753)
XLA Ops:
  7.2 0.0 all-gather.5.cloned.1.call-start
  7.2 18.9 %all_gather.10 = bf16[768,512]{1,0:T(8,128)(2,1)} all-gather(bf16[768,128]{1,0:T(8,128)(2,1)} %param.3), channel_id=1, replica_groups=mesh['dp_0'=4,'dp_1'=2,'tensor_0'=8,'tensor_1'=4] {'tensor_1'}, dimensions={1}, use_global_device_ids=true | all-gather | bytes 983040 | tf_op jit(solution)/shard_map/all_gather | solution.py:15
  26.1 0.0 all-gather.5.cloned.1.call-update
  26.2 0.0 all-gather.3.cloned.1.call-start
  26.2 0.7 all-gather.3.cloned.1.call-update
  27.0 73.0 %all-gather.5.cloned.1.call-done = bf16[768,4096]{1,0:T(8,128)(2,1)} async-done(((bf16[768,512]{1,0:T(8,128)(2,1)}), bf16[768,4096]{1,0:T(8,128)(2,1)}) %all-gather.5.cloned.1.call-update) | async-done | bytes 6291472 | tf_op jit(solution)/shard_map/all_gather | solution.py:15
  100.0 89.7 %all-gather.3.cloned.1.call-done = bf16[2048,4096]{1,0:T(8,128)(2,1)} async-done(((bf16[2048,512]{1,0:T(8,128)(2,1)}), bf16[2048,4096]{1,0:T(8,128)(2,1)}) %all-gather.3.cloned.1.call-update) | async-done | bytes 16777232 | tf_op jit(solution)/shard_map/all_gather | solution.py:65
  189.7 18.3 %fusion.3 = f32[2048,768]{1,0:T(8,128)S(1)} fusion(bf16[2048,4096]{1,0:T(8,128)(2,1)} %all-gather.3.cloned.1.call-done, bf16[768,4096]{1,0:T(8,128)(2,1)} %all-gather.5.cloned.1.call-done), kind=kOutput, calls=%fused_computation.26 | convolution fusion | flops 12884901888 | bytes 29360128 | tf_op jit(solution)/shard_map/dot_general | solution.py:64
  208.0 0.0 copy-start
  208.0 0.0 copy-start.1
  208.0 0.3 slice_reduce_fusion.1
  208.3 2.3 copy-done
  210.7 0.1 reduce_max.60
  210.7 0.1 reduce_max.58
  210.8 0.1 reduce_max.54
  210.9 0.1 reduce_max.56
  211.0 0.0 copy-done.1
  211.0 3.7 %exponential_reduce_fusion.3 = (f32[768]{0:T(1024)S(1)}, f32[768]{0:T(1024)S(1)}, f32[768]{0:T(1024)S(1)}, f32[768]{0:T(1024)S(1)}, f32[768]{0:T(1024)S(1)}, /*i...) fusion(f32[2048,768]{1,0:T(8,128)} %copy-done, f32[768]{0:T(1024)S(1)} %get-tuple-element.17, ...), kind=kLoop, calls=%fused_computation.7 | loop fusion | flops 7858176 | bytes 6339584 | tf_op jit(solution)/shard_map/reduce_sum | solution.py:50
  214.7 0.1 add.98
  214.8 0.1 reduce_sum.114
  214.9 0.1 reduce_sum.112
  215.0 0.1 reduce_sum.110
  215.0 0.1 reduce_sum.108
  215.2 0.1 pad_maximum_fusion
  215.3 18.5 %all_to_all.12 = f32[32,1,72]{2,1,0:T(1,128)S(1)} all-to-all(f32[32,1,72]{2,1,0:T(1,128)S(1)} %bitcast.8), channel_id=1, replica_groups=mesh['dp_0'=4,'dp_1'=2,'tensor_0'=8,'tensor_1'=4] {'tensor_0','tensor_1'}, dimensions={0} | all-to-all | bytes 18432 | tf_op jit(solution)/shard_map/all_to_all | solution.py:22
  233.8 0.1 fusion
  233.9 1.1 fusion.1
  235.0 9.8 %psum.28 = f32[]{:T(128)} all-reduce(f32[]{:T(128)} %get-tuple-element.20), channel_id=1, replica_groups=mesh['dp_0'=4,'dp_1'=2,'tensor_0'=8,'tensor_1'=4] {'dp_0'}, use_global_device_ids=true, to_apply=%region_16.17 | all-reduce | flops 1 | bytes 8 | tf_op jit(solution)/shard_map/psum | solution.py:34
  244.8 3.1 %psum.29 = f32[]{:T(128)} all-reduce(f32[]{:T(128)} %psum.28), channel_id=1, replica_groups=mesh['dp_0'=4,'dp_1'=2,'tensor_0'=8,'tensor_1'=4] {'dp_1'}, use_global_device_ids=true, to_apply=%region_17.18 | all-reduce | flops 1 | bytes 8 | tf_op jit(solution)/shard_map/psum | solution.py:34
  247.8 16.1 %psum.30 = f32[]{:T(128)} all-reduce(f32[]{:T(128)} %psum.29), channel_id=1, replica_groups=mesh['dp_0'=4,'dp_1'=2,'tensor_0'=8,'tensor_1'=4] {'tensor_0'}, use_global_device_ids=true, to_apply=%region_18.19 | all-reduce | flops 1 | bytes 8 | tf_op jit(solution)/shard_map/psum | solution.py:34
  264.0 9.6 %psum.31 = f32[]{:T(128)} all-reduce(f32[]{:T(128)} %psum.30), channel_id=1, replica_groups=mesh['dp_0'=4,'dp_1'=2,'tensor_0'=8,'tensor_1'=4] {'tensor_1'}, use_global_device_ids=true, to_apply=%region_19.20 | all-reduce | flops 1 | bytes 8 | tf_op jit(solution)/shard_map/psum | solution.py:34
  (6 shorter events, 0.1 us)
Async XLA Ops:
  7.2 92.8 %all-gather.5.cloned.1.call-start = ((), (), s32[]{:S(2)}) async-start(), calls=%async_computation.2 | async-start | bytes 7077888 | tf_op jit(solution)/shard_map/all_gather | solution.py:15
  26.2 163.5 %all-gather.3.cloned.1.call-start = ((), (), s32[]{:S(2)}) async-start(), calls=%async_computation.1 | async-start | bytes 18874368 | tf_op jit(solution)/shard_map/all_gather | solution.py:65
  208.0 2.7 copy-start
  208.0 3.0 %copy-start.1 = (s32[768]{0:T(1024)S(1)}, s32[768]{0:T(1024)}, u32[]{:S(2)}) copy-start(s32[768]{0:T(1024)} %param.5) | copy-start | bytes 9220
Sparse Core Ops, SparseCore 0:
  26.3 73.6 all-gather.4
  101.8 87.7 all-gather.2
where the time goes:
time: 282 us
  waiting for transfers between devices  163 us (58%)
  blocking collectives  76 us (27%)
  matrix products  18.3 us (6%)
  between operations  16 us (6%)
  other arithmetic  5.37 us (2%)
  local copies, waits for them, and re-layouts  3.03 us (1%)
    all_gather x1, waiting for transfers between devices, body(): lax.all_gather(out_embed, DP, axis=1, tiled=True)  89.7 us
    all_gather x1, waiting for transfers between devices, whole_of(): shard = lax.all_gather(shard, axis, axis=dim, tiled=True)  73 us
    psum x4, blocking collectives, one_axis_at_a_time(): shard = lax.psum(shard, axis)  38.5 us
    all_gather x1, blocking collectives, whole_of(): shard = lax.all_gather(shard, axis, axis=dim, tiled=True)  18.9 us
    all_to_all x1, blocking collectives, side_by_side(): lax.all_to_all(both, axis, split_axis=split_dim, concat_axis=concat_dim,...  18.5 us
    dot_general x1, matrix products, body(): lax.dot_general(lax.all_gather(out_embed, DP, axis=1, tiled=True), full_h...  18.3 us
  transfers between devices with their start and end apart: 2, of which 2 were waited for; matrix products, arithmetic and copies ran while one was open for 0% of the time, Pallas kernels for 0%

commit v1 on v0

--- a/solution.py
+++ b/solution.py
@@ -62,7 +62,9 @@
     vocab_offset = lax.axis_index(TENSOR) * vocab_rows
     block_count = vocab_rows // BLOCK
     all_logits = lax.dot_general(
-        lax.all_gather(out_embed, DP, axis=1, tiled=True),
+        jnp.concatenate(
+            lax.all_to_all(jnp.stack([out_embed] * lax.axis_size(DP)), DP, 0, 0), axis=1
+        ),
         full_hidden,
         (((1,), (1,)), ((), ())),
         preferred_element_type=jnp.float32,

time: 282 us -> 300 us (1.064)
  local copies, waits for them, and re-layouts: 3.03 us -> 11.9 us
  starting transfers between devices: 0.08 us -> 5.93 us
  waiting for transfers between devices: 163 us -> 166 us
    all_to_all x0 -> x1, waiting for transfers between devices: none -> 91.6 us  [body(): lax.all_to_all(jnp.stack([out_embed] * lax.axis_size(DP)), DP, 0, 0)]
    all_gather x1 -> x0, waiting for transfers between devices: 89.7 us -> none  [body(): lax.all_gather(out_embed, DP, axis=1, tiled=True)]
    another operation x0 -> x1, local copies, waits for them, and re-layouts: none -> 5.98 us  [body(): jnp.stack([out_embed] * lax.axis_size(DP))]
    all_to_all x0 -> x1, starting transfers between devices: none -> 5.89 us  [body(): lax.all_to_all(jnp.stack([out_embed] * lax.axis_size(DP)), DP, 0, 0)]
where the time goes in v1:
time: 300 us
  waiting for transfers between devices  166 us (55%)
  blocking collectives  76.2 us (25%)
  matrix products  18 us (6%)
  between operations  16 us (5%)
  local copies, waits for them, and re-layouts  11.9 us (4%)
  starting transfers between devices  5.93 us (2%)
  other arithmetic  5.37 us (2%)
    all_to_all x1, waiting for transfers between devices, body(): lax.all_to_all(jnp.stack([out_embed] * lax.axis_size(DP)), DP, 0, 0)  91.6 us
    all_gather x1, waiting for transfers between devices, whole_of(): shard = lax.all_gather(shard, axis, axis=dim, tiled=True)  74.6 us
    psum x4, blocking collectives, one_axis_at_a_time(): shard = lax.psum(shard, axis)  38.3 us
    all_to_all x1, blocking collectives, side_by_side(): lax.all_to_all(both, axis, split_axis=split_dim, concat_axis=concat_dim,...  19.7 us
    all_gather x1, blocking collectives, whole_of(): shard = lax.all_gather(shard, axis, axis=dim, tiled=True)  18.1 us
    dot_general x1, matrix products, body(): lax.dot_general(jnp.concatenate(lax.all_to_all(jnp.stack([out_embed] * la...  18 us
  transfers between devices with their start and end apart: 2, of which 2 were waited for; matrix products, arithmetic and copies ran while one was open for 0% of the time, Pallas kernels for 0%

profile of v1, /device:TPU:32, one launch (start us, length us, event | category | flops | bytes accessed | tf_op | source)
XLA Modules:
  0.0 299.6 jit_solution(14374093533055395081)
XLA Ops:
  7.2 2.9 copy.6
  10.1 6.0 %stack.2 = bf16[8,2048,512]{1,2,0:T(8,128)(2,1)} broadcast(bf16[2048,512]{0,1:T(8,128)(2,1)S(1)} %copy.6), dimensions={1,2} | broadcast | bytes 18874368 | tf_op jit(solution)/shard_map/stack | solution.py:66
  16.1 5.9 %all-to-all-start = ((bf16[8,2048,512]{1,2,0:T(8,128)(2,1)}), bf16[8,2048,512]{1,2,0:T(8,128)(2,1)}, u32[]{:S(2)}, u32[]{:S(2)}) async-start(bf16[8,2048,512]{1,2,0:T(8,128)(2,1)} %stack.2), calls=%async_computation | async-start | bytes 33554432 | tf_op jit(solution)/shard_map/all_to_all | solution.py:66
  22.0 0.0 all-gather.2.cloned.1.call-start
  22.0 0.0 copy-done.1
  22.0 18.1 %all_gather.6 = bf16[768,512]{1,0:T(8,128)(2,1)} all-gather(bf16[768,128]{1,0:T(8,128)(2,1)S(1)} %copy-done.1), channel_id=1, replica_groups=mesh['dp_0'=4,'dp_1'=2,'tensor_0'=8,'tensor_1'=4] {'tensor_1'}, dimensions={1}, use_global_device_ids=true | all-gather | bytes 983040 | tf_op jit(solution)/shard_map/all_gather | solution.py:15
  40.2 0.0 all-gather.2.cloned.1.call-update
  40.2 74.6 %all-gather.2.cloned.1.call-done = bf16[768,4096]{1,0:T(8,128)(2,1)} async-done(((bf16[768,512]{1,0:T(8,128)(2,1)}), bf16[768,4096]{1,0:T(8,128)(2,1)}) %all-gather.2.cloned.1.call-update) | async-done | bytes 6291472 | tf_op jit(solution)/shard_map/all_gather | solution.py:15
  114.8 91.6 %all-to-all-done = bf16[8,2048,512]{1,2,0:T(8,128)(2,1)} async-done(((bf16[8,2048,512]{1,2,0:T(8,128)(2,1)}), bf16[8,2048,512]{1,2,0:T(8,128)(2,1)}, u32[]{:S(2)}, u32[]{:S(2)}) %all-to-all-start) | async-done | bytes 16777248 | tf_op jit(solution)/shard_map/all_to_all | solution.py:66
  206.4 18.0 %fusion.3 = f32[2048,768]{1,0:T(8,128)S(1)} fusion(bf16[2048,4096]{0,1:T(8,128)(2,1)} %bitcast.1, bf16[768,4096]{1,0:T(8,128)(2,1)} %all-gather.2.cloned.1.call-done), kind=kOutput, calls=%fused_computation.26 | convolution fusion | flops 12884901888 | bytes 29360128 | tf_op jit(solution)/shard_map/dot_general | solution.py:64
  224.4 0.0 copy-start
  224.4 0.0 copy-start.2
  224.4 0.3 slice_reduce_fusion.1
  224.8 2.3 copy-done
  227.1 0.1 reduce_max.60
  227.2 0.1 reduce_max.58
  227.3 0.1 reduce_max.54
  227.3 0.1 reduce_max.56
  227.4 3.7 %exponential_reduce_fusion.3 = (f32[768]{0:T(1024)S(1)}, f32[768]{0:T(1024)S(1)}, f32[768]{0:T(1024)S(1)}, f32[768]{0:T(1024)S(1)}, f32[768]{0:T(1024)S(1)}, /*i...) fusion(f32[2048,768]{1,0:T(8,128)} %copy-done, f32[768]{0:T(1024)S(1)} %get-tuple-element.17, ...), kind=kLoop, calls=%fused_computation.7 | loop fusion | flops 7858176 | bytes 6339584 | tf_op jit(solution)/shard_map/reduce_sum | solution.py:50
  231.1 0.1 add.98
  231.2 0.1 reduce_sum.114
  231.3 0.1 reduce_sum.112
  231.4 0.1 reduce_sum.110
  231.5 0.1 reduce_sum.108
  231.6 0.1 pad_maximum_fusion
  231.7 19.7 %all_to_all.17 = f32[32,1,72]{2,1,0:T(1,128)S(1)} all-to-all(f32[32,1,72]{2,1,0:T(1,128)S(1)} %bitcast.11), channel_id=1, replica_groups=mesh['dp_0'=4,'dp_1'=2,'tensor_0'=8,'tensor_1'=4] {'tensor_0','tensor_1'}, dimensions={0} | all-to-all | bytes 18432 | tf_op jit(solution)/shard_map/all_to_all | solution.py:22
  251.5 0.1 fusion
  251.5 1.1 fusion.1
  252.7 9.5 %psum.28 = f32[]{:T(128)} all-reduce(f32[]{:T(128)} %get-tuple-element.20), channel_id=1, replica_groups=mesh['dp_0'=4,'dp_1'=2,'tensor_0'=8,'tensor_1'=4] {'dp_0'}, use_global_device_ids=true, to_apply=%region_16.17 | all-reduce | flops 1 | bytes 8 | tf_op jit(solution)/shard_map/psum | solution.py:34
  262.2 3.1 %psum.29 = f32[]{:T(128)} all-reduce(f32[]{:T(128)} %psum.28), channel_id=1, replica_groups=mesh['dp_0'=4,'dp_1'=2,'tensor_0'=8,'tensor_1'=4] {'dp_1'}, use_global_device_ids=true, to_apply=%region_17.18 | all-reduce | flops 1 | bytes 8 | tf_op jit(solution)/shard_map/psum | solution.py:34
  265.2 16.2 %psum.30 = f32[]{:T(128)} all-reduce(f32[]{:T(128)} %psum.29), channel_id=1, replica_groups=mesh['dp_0'=4,'dp_1'=2,'tensor_0'=8,'tensor_1'=4] {'tensor_0'}, use_global_device_ids=true, to_apply=%region_18.19 | all-reduce | flops 1 | bytes 8 | tf_op jit(solution)/shard_map/psum | solution.py:34
  281.4 9.6 %psum.31 = f32[]{:T(128)} all-reduce(f32[]{:T(128)} %psum.30), channel_id=1, replica_groups=mesh['dp_0'=4,'dp_1'=2,'tensor_0'=8,'tensor_1'=4] {'tensor_1'}, use_global_device_ids=true, to_apply=%region_19.20 | all-reduce | flops 1 | bytes 8 | tf_op jit(solution)/shard_map/psum | solution.py:34
  (8 shorter events, 0.1 us)
Async XLA Ops:
  16.1 6.0 %copy-start.1 = (bf16[768,128]{1,0:T(8,128)(2,1)S(1)}, bf16[768,128]{1,0:T(8,128)(2,1)}, u32[]{:S(2)}) copy-start(bf16[768,128]{1,0:T(8,128)(2,1)} %param.3) | copy-start | bytes 589828
  16.1 190.4 %all-to-all-start = ((bf16[8,2048,512]{1,2,0:T(8,128)(2,1)}), bf16[8,2048,512]{1,2,0:T(8,128)(2,1)}, u32[]{:S(2)}, u32[]{:S(2)}) async-start(bf16[8,2048,512]{1,2,0:T(8,128)(2,1)} %stack.2), calls=%async_computation | async-start | bytes 33554432 | tf_op jit(solution)/shard_map/all_to_all | solution.py:66
  22.0 92.8 %all-gather.2.cloned.1.call-start = ((), (), s32[]{:S(2)}) async-start(), calls=%async_computation.2 | async-start | bytes 7077888 | tf_op jit(solution)/shard_map/all_gather | solution.py:15
  224.4 2.7 copy-start
  224.4 3.0 copy-start.2
Sparse Core Ops, SparseCore 0:
  40.3 74.4 all-gather.1
